TPU v7x, 32 devices: a whole 2x2x4 slice. The times are simulated.
32 devices in a mesh: rep: 4 (over y, x), fsdp: 8 (over z, core).
Axes of the slice: x: 2, y: 2, z: 4, core: 2. Of those that a mesh axis runs over, the one named last changes fastest.
Arguments:
- momentum: float32 [4, 18432, 2304], P('rep', 'fsdp'), may hold values from -60 to 60
- gradient: bfloat16 [4, 18432, 2304], P('rep', 'fsdp'), may hold values from -30 to 30
- right_factor: float32 [2304, 256], P('fsdp'), may hold values from -0.125 to 0.125
Outputs:
- new_momentum: float32 [4, 18432, 2304], P('rep', 'fsdp')
- update: bfloat16 [18432, 2304], P('fsdp')
- new_factor: float32 [2304, 256], P('fsdp')
All inputs are finite; a program needn't handle non-finite values.
Results may differ from a plain program's by a relative error of at most 0.001.
Values sent between devices are 32-bit elements; how exact they have to be, the bound alone decides.
A program may use at most 128 MiB of HBM per device.

v0:
```python
import functools
import math

import jax
import jax.numpy as jnp
from jax import lax
from jax.experimental import pallas as pl
from jax.experimental.pallas import tpu as pltpu
from jax.sharding import PartitionSpec as P

epsilon = 1e-06
decay_rate = 0.95
highest = lax.Precision.HIGHEST
f32 = jnp.float32
bf16 = jnp.bfloat16
MESH = pl.DeviceIdType.MESH
VMEM_LIMIT = 60 * 1024 * 1024


def split(x):
    high = x.astype(bf16)
    return high, (x - high.astype(f32)).astype(bf16)


def dot(a, b, dims=(((1,), (0,)), ((), ()))):
    return lax.dot_general(a, b, dims, preferred_element_type=f32)


def exact(a, b, dims=(((1,), (0,)), ((), ()))):
    return lax.dot_general(a, b, dims, precision=highest, preferred_element_type=f32)


NT = (((1,), (1,)), ((), ()))
TN = (((0,), (0,)), ((), ()))


def greet(peers):
    barrier = pltpu.get_barrier_semaphore()
    for peer in peers:
        pl.semaphore_signal(barrier, inc=1, device_id=peer, device_id_type=MESH)
    pl.semaphore_wait(barrier, len(peers))


def remote(src, dst, send_sem, recv_sem, peer):
    copy = pltpu.make_async_remote_copy(
        src_ref=src, dst_ref=dst, send_sem=send_sem, recv_sem=recv_sem,
        device_id=peer, device_id_type=MESH,
    )
    copy.start()
    return copy


def gather_right(shard_n, own_ref, full_ref, send, recv, fsend, frecv, local):
    f = lax.axis_index("fsdp")
    r = lax.axis_index("rep")
    rows = own_ref.shape[0]
    chips = shard_n // 2
    chip, core = f // 2, lax.rem(f, 2)
    mate = (r, chip * 2 + 1 - core)
    others = [(r, lax.rem(chip + k, chips) * 2 + core) for k in range(1, chips)]
    greet([mate] + others)

    def block(index):
        return full_ref.at[pl.ds(pl.multiple_of(index * rows, 8), rows)]

    own = pltpu.make_async_copy(own_ref, block(f), local)
    own.start()
    copies = [remote(own_ref, block(f), send.at[k], recv.at[k], others[k]) for k in range(chips - 1)]
    passed = [remote(own_ref, block(f), fsend.at[0], frecv.at[0], mate)]
    for k in reversed(range(chips - 1)):
        copies[k].wait_recv()
        source = lax.rem(chip - (k + 1) + chips, chips) * 2 + core
        passed.append(remote(block(source), block(source), fsend.at[k + 1], frecv.at[k + 1], mate))
    for copy in copies:
        copy.wait_send()
    for copy in passed:
        copy.wait()
    own.wait()


def project(m_ref, g_ref, right_ref, out_ref, high, low):
    @pl.when(pl.program_id(0) == 0)
    def _():
        high[...], low[...] = split(right_ref[...])

    bh, bl = split(m_ref[0] + g_ref[0].astype(f32))
    out_ref[...] = dot(bh, high[...]) + dot(bh, low[...]) + dot(bl, high[...])


def inverse_small(a, size):
    row = lax.broadcasted_iota(jnp.int32, (size, 2 * size), 0)
    lane = lax.broadcasted_iota(jnp.int32, (size, 2 * size), 1)
    eye = jnp.where(row == lane - size, 1.0, 0.0).astype(f32)
    work = jnp.concatenate([a, eye[:, size:]], axis=1)
    for j in range(size):
        first = (j // 8) * 8
        pivot = work[j:j + 1, :]
        scaled = pivot / work[j:j + 1, j:j + 1]
        tail = work[first:, :]
        below = row[first:, :] > j
        tail = tail - jnp.where(below, tail[:, j:j + 1], 0.0) * scaled
        work = tail if first == 0 else jnp.concatenate([work[:first], tail], axis=0)
    diag = jnp.sum(jnp.where(row == lane, work, 0.0), axis=1, keepdims=True)
    return work[:, size:] * (1.0 / jnp.sqrt(diag))


def inverse_lower(a, size):
    if size <= 64:
        return inverse_small(a, size)
    h = size // 2
    top = inverse_lower(a[:h, :h], h)
    cross = exact(a[h:, :h], top, NT)
    low = inverse_lower(a[h:, h:] - exact(cross, cross, NT), h)
    corner = -exact(low, exact(cross, top))
    return jnp.concatenate(
        [jnp.concatenate([top, jnp.zeros((h, h), f32)], axis=1),
         jnp.concatenate([corner, low], axis=1)], axis=0)


def orthonormalize(reps, shard_n, part_ref, q_ref, full, xin, yin, xin2, yin2, gout, gin, gfull, inv,
                   send, recv, gsend, grecv, asend, arecv):
    r = lax.axis_index("rep")
    f = lax.axis_index("fsdp")
    rows, rank = part_ref.shape
    chunk = rows // reps
    half = rank // 2
    total = reps * shard_n
    me = r * shard_n + f
    sx = 1 - 2 * lax.rem(r, 2)
    sy = 1 - 2 * (r // 2)
    px, py, pd = r + sx, r + 2 * sy, r + sx + 2 * sy
    left, right = pl.ds(0, half), pl.ds(half, half)

    def of(index):
        return pl.ds(pl.multiple_of(index * chunk, 8), chunk)

    def device(k):
        d = lax.rem(me + k, total)
        return d, (d // shard_n, lax.rem(d, shard_n))

    peers = [device(k) for k in range(1, total)]
    greet([peer for _, peer in peers])

    s1 = [
        remote(part_ref.at[of(pd), left], xin.at[0], send.at[0], recv.at[0], (px, f)),
        remote(part_ref.at[of(pd), right], yin.at[0], send.at[1], recv.at[1], (py, f)),
        remote(part_ref.at[of(px), left], xin.at[1], send.at[2], recv.at[2], (px, f)),
        remote(part_ref.at[of(py), right], yin.at[1], send.at[3], recv.at[3], (py, f)),
    ]
    s1[0].wait_recv()
    xin[0] = xin[0] + part_ref[of(py), left]
    a = remote(xin.at[0], xin2, send.at[4], recv.at[4], (py, f))
    s1[1].wait_recv()
    yin[0] = yin[0] + part_ref[of(px), right]
    b = remote(yin.at[0], yin2, send.at[5], recv.at[5], (px, f))
    s1[2].wait_recv()
    xin[1] = xin[1] + part_ref[of(r), left]
    s1[3].wait_recv()
    yin[1] = yin[1] + part_ref[of(r), right]
    a.wait_recv()
    full[of(r), left] = xin[1] + xin2[...]
    b.wait_recv()
    full[of(r), right] = yin[1] + yin2[...]

    own = full[of(r), :]
    piece = rank // total
    gout[...] = exact(own, own, TN)

    def rows_of(index):
        return pl.ds(pl.multiple_of(index * piece, 8), piece)

    g1 = [
        remote(gout.at[rows_of(d)], gin.at[k], gsend.at[k], grecv.at[k], peer)
        for k, (d, peer) in enumerate(peers)
    ]
    acc = gout[rows_of(me), :]
    for k in range(total - 1):
        g1[k].wait_recv()
        acc = acc + gin[k]
    gfull[rows_of(me), :] = acc
    g2 = [
        remote(gfull.at[rows_of(me)], gfull.at[rows_of(me)], asend.at[k], arecv.at[k], peer)
        for k, (d, peer) in enumerate(peers)
    ]
    t1 = [
        remote(full.at[of(r), left], full.at[of(r), left], send.at[6], recv.at[6], (px, f)),
        remote(full.at[of(r), right], full.at[of(r), right], send.at[7], recv.at[7], (py, f)),
        remote(full.at[of(r), right], full.at[of(r), right], send.at[8], recv.at[8], (px, f)),
        remote(full.at[of(r), left], full.at[of(r), left], send.at[9], recv.at[9], (py, f)),
    ]
    for copy in g2:
        copy.wait_recv()
    t1[0].wait_recv()
    t2 = [remote(full.at[of(px), left], full.at[of(px), left], send.at[10], recv.at[10], (py, f))]
    t1[1].wait_recv()
    t2.append(remote(full.at[of(py), right], full.at[of(py), right], send.at[11], recv.at[11], (px, f)))
    inv[...] = inverse_lower(gfull[...], rank)
    t1[2].wait_recv()
    t1[3].wait_recv()
    t2[0].wait_recv()
    t2[1].wait_recv()
    for copy in s1 + [a, b] + g1 + g2 + t1 + t2:
        copy.wait_send()
    step = 256 if rows % 256 == 0 else chunk

    @pl.loop(0, rows // step)
    def _(i):
        at = pl.ds(pl.multiple_of(i * step, 8), step)
        q_ref[at, :] = exact(full[at, :], inv[...], NT)


def factor_term(m_ref, g_ref, q_ref, out_ref):
    bh, bl = split(m_ref[0] + g_ref[0].astype(f32))
    qh, ql = split(q_ref[...].T)
    term = dot(jnp.concatenate([qh, qh, ql], axis=1), jnp.concatenate([bh, bl, bh], axis=0))

    @pl.when(pl.program_id(0) == 0)
    def _():
        out_ref[...] = term

    @pl.when(pl.program_id(0) != 0)
    def _():
        out_ref[...] += term


def sum_factor(reps, shard_n, part_ref, out_ref, cin, xin, yin, xin2, yin2, zin, zsum, send, recv, zsend, zrecv):
    r = lax.axis_index("rep")
    f = lax.axis_index("fsdp")
    chips = shard_n // 2
    chip, core = f // 2, lax.rem(f, 2)
    rank, cols = part_ref.shape
    half = cols // 2
    left, right = pl.ds(0, half), pl.ds(half, half)
    sx = 1 - 2 * lax.rem(r, 2)
    sy = 1 - 2 * (r // 2)
    px, py, pd = r + sx, r + 2 * sy, r + sx + 2 * sy
    n0 = rank // 2
    n1 = n0 // reps
    n2 = n1 // chips
    mate = (r, chip * 2 + 1 - core)
    zs = [lax.rem(chip + k, chips) for k in range(1, chips)]
    greet([mate, (px, f), (py, f)] + [(r, z * 2 + core) for z in zs])

    def of(index):
        return pl.ds(pl.multiple_of(index * n1, 8), n1)

    mine = core * n0
    order = [pd, px, py, r]
    c = []
    for k, which in enumerate(order):
        away = pl.ds(pl.multiple_of((1 - core) * n0 + which * n1, 8), n1)
        c.append(remote(part_ref.at[away], cin.at[of(which)], send.at[k], recv.at[k], mate))

    def add_own(which):
        at = pl.ds(pl.multiple_of(mine + which * n1, 8), n1)
        cin[of(which), :] = cin[of(which), :] + part_ref[at, :]

    c[0].wait_recv()
    add_own(pd)
    s1 = [
        remote(cin.at[of(pd), left], xin.at[0], send.at[4], recv.at[4], (px, f)),
        remote(cin.at[of(pd), right], yin.at[0], send.at[5], recv.at[5], (py, f)),
    ]
    c[1].wait_recv()
    add_own(px)
    s1.append(remote(cin.at[of(px), left], xin.at[1], send.at[6], recv.at[6], (px, f)))
    c[2].wait_recv()
    add_own(py)
    s1.append(remote(cin.at[of(py), right], yin.at[1], send.at[7], recv.at[7], (py, f)))
    c[3].wait_recv()
    add_own(r)
    s1[0].wait_recv()
    xin[0] = xin[0] + cin[of(py), left]
    a = remote(xin.at[0], xin2, send.at[8], recv.at[8], (py, f))
    s1[1].wait_recv()
    yin[0] = yin[0] + cin[of(px), right]
    b = remote(yin.at[0], yin2, send.at[9], recv.at[9], (px, f))
    s1[2].wait_recv()
    xin[1] = xin[1] + cin[of(r), left]
    s1[3].wait_recv()
    yin[1] = yin[1] + cin[of(r), right]
    a.wait_recv()
    zsum[:, left] = xin[1] + xin2[...]
    b.wait_recv()
    zsum[:, right] = yin[1] + yin2[...]
    z1 = []
    for k, z in enumerate(zs):
        rows = pl.ds(pl.multiple_of(z * n2, 8), n2)
        z1.append(remote(zsum.at[rows], zin.at[k], zsend.at[k], zrecv.at[k], (r, z * 2 + core)))
    acc = zsum[pl.ds(pl.multiple_of(chip * n2, 8), n2), :]
    for k in range(chips - 1):
        z1[k].wait_recv()
        acc = acc + zin[k]

    def block(rep, z, co):
        return pl.ds(pl.multiple_of(co * n0 + rep * n1 + z * n2, 8), n2)

    def group(rep, co):
        return pl.ds(pl.multiple_of(co * n0 + rep * n1, 8), n1)

    at = block(r, chip, core)
    out_ref[at, :] = acc * (1.0 / reps)
    z2 = [
        remote(out_ref.at[at], out_ref.at[at], zsend.at[chips + k], zrecv.at[chips + k], (r, z * 2 + core))
        for k, z in enumerate(zs)
    ]
    for copy in z2:
        copy.wait_recv()
    whole = group(r, core)
    t = [
        remote(out_ref.at[whole, left], out_ref.at[whole, left], send.at[10], recv.at[10], (px, f)),
        remote(out_ref.at[whole, right], out_ref.at[whole, right], send.at[11], recv.at[11], (py, f)),
        remote(out_ref.at[whole, right], out_ref.at[whole, right], send.at[12], recv.at[12], (px, f)),
        remote(out_ref.at[whole, left], out_ref.at[whole, left], send.at[13], recv.at[13], (py, f)),
        remote(out_ref.at[whole], out_ref.at[whole], send.at[14], recv.at[14], mate),
    ]
    t[0].wait_recv()
    gx, gy, gd = group(px, core), group(py, core), group(pd, core)
    t.append(remote(out_ref.at[gx, left], out_ref.at[gx, left], send.at[15], recv.at[15], (py, f)))
    t[1].wait_recv()
    t.append(remote(out_ref.at[gy, right], out_ref.at[gy, right], send.at[16], recv.at[16], (px, f)))
    t[2].wait_recv()
    t.append(remote(out_ref.at[gx], out_ref.at[gx], send.at[17], recv.at[17], mate))
    t[3].wait_recv()
    t.append(remote(out_ref.at[gy], out_ref.at[gy], send.at[18], recv.at[18], mate))
    t[5].wait_recv()
    t[6].wait_recv()
    t.append(remote(out_ref.at[gd], out_ref.at[gd], send.at[19], recv.at[19], mate))
    for index in (4, 7, 8, 9):
        t[index].wait_recv()
    for copy in c + s1 + [a, b] + z1 + z2 + t:
        copy.wait_send()


def finish(scale, m_ref, g_ref, q_ref, factor_ref, mom_ref, upd_ref, new_ref, plain, pieces):
    @pl.when(pl.program_id(0) == 0)
    def _():
        factor = factor_ref[...]
        norms = jnp.sqrt(jnp.sum(factor * factor, axis=1, keepdims=True) + epsilon)
        new = factor / norms
        new_ref[...] = new
        plain[...] = ((1.0 - decay_rate) * factor).astype(bf16)
        high, low = split(new)
        pieces[...] = jnp.concatenate([high, low, high], axis=0)

    qh, ql = split(q_ref[...])
    mom_ref[0] = (m_ref[0] + g_ref[0].astype(f32)) - dot(qh, plain[...])
    direction = dot(jnp.concatenate([qh, qh, ql], axis=1), pieces[...])
    upd_ref[...] = (scale * direction).astype(bf16)


def params(**more):
    return pltpu.CompilerParams(vmem_limit_bytes=VMEM_LIMIT, **more)


def by_kernels(reps, shard_n, total_rows, momentum, gradient, right_factor):
    _, rows, cols = momentum.shape
    rank = right_factor.shape[1]
    tile = 256 if rows % 256 == 0 else rows // 8
    steps = rows // tile
    vmem = pl.BlockSpec(memory_space=pltpu.VMEM)
    dma = pltpu.SemaphoreType.DMA
    chips = shard_n // 2

    def stripe(width):
        return pl.BlockSpec((tile, width), lambda i: (i, 0))

    cube = pl.BlockSpec((1, tile, cols), lambda i: (0, i, 0))

    def fixed(*shape):
        return pl.BlockSpec(shape, lambda i: (0,) * len(shape))

    right = pl.pallas_call(
        functools.partial(gather_right, shard_n),
        out_shape=jax.ShapeDtypeStruct((cols, rank), f32),
        in_specs=[vmem], out_specs=vmem,
        scratch_shapes=[dma((chips,)), dma((chips,)), dma((chips,)), dma((chips,)), dma],
        compiler_params=params(collective_id=0, has_side_effects=True),
        name="gather_right",
    )(right_factor)
    partial = pl.pallas_call(
        project,
        grid=(steps,),
        out_shape=jax.ShapeDtypeStruct((rows, rank), f32),
        in_specs=[cube, cube, fixed(cols, rank)], out_specs=stripe(rank),
        scratch_shapes=[pltpu.VMEM((cols, rank), bf16)] * 2,
        compiler_params=params(), name="project",
    )(momentum, gradient, right)
    chunk, total = rows // reps, reps * shard_n
    orthonormal = pl.pallas_call(
        functools.partial(orthonormalize, reps, shard_n),
        out_shape=jax.ShapeDtypeStruct((rows, rank), f32),
        in_specs=[vmem], out_specs=vmem,
        scratch_shapes=[
            pltpu.VMEM((rows, rank), f32),
            pltpu.VMEM((2, chunk, rank // 2), f32), pltpu.VMEM((2, chunk, rank // 2), f32),
            pltpu.VMEM((chunk, rank // 2), f32), pltpu.VMEM((chunk, rank // 2), f32),
            pltpu.VMEM((rank, rank), f32),
            pltpu.VMEM((total, rank // total, rank), f32),
            pltpu.VMEM((rank, rank), f32), pltpu.VMEM((rank, rank), f32),
            dma((12,)), dma((12,)), dma((total,)), dma((total,)), dma((total,)), dma((total,)),
        ],
        compiler_params=params(collective_id=1, has_side_effects=True),
        name="orthonormalize",
    )(partial)
    term = pl.pallas_call(
        factor_term,
        grid=(steps,),
        out_shape=jax.ShapeDtypeStruct((rank, cols), f32),
        in_specs=[cube, cube, stripe(rank)], out_specs=fixed(rank, cols),
        compiler_params=params(), name="factor_term",
    )(momentum, gradient, orthonormal)
    n1 = rank // 2 // reps
    factor = pl.pallas_call(
        functools.partial(sum_factor, reps, shard_n),
        out_shape=jax.ShapeDtypeStruct((rank, cols), f32),
        in_specs=[vmem], out_specs=vmem,
        scratch_shapes=[
            pltpu.VMEM((rank // 2, cols), f32),
            pltpu.VMEM((2, n1, cols // 2), f32), pltpu.VMEM((2, n1, cols // 2), f32),
            pltpu.VMEM((n1, cols // 2), f32), pltpu.VMEM((n1, cols // 2), f32),
            pltpu.VMEM((chips, n1 // chips, cols), f32), pltpu.VMEM((n1, cols), f32),
            dma((20,)), dma((20,)), dma((2 * chips,)), dma((2 * chips,)),
        ],
        compiler_params=params(collective_id=2, has_side_effects=True),
        name="sum_factor",
    )(term)
    new_momentum, update, new = pl.pallas_call(
        functools.partial(finish, math.sqrt(total_rows * cols / rank)),
        grid=(steps,),
        out_shape=(
            jax.ShapeDtypeStruct(momentum.shape, f32),
            jax.ShapeDtypeStruct((rows, cols), bf16),
            jax.ShapeDtypeStruct((rank, cols), f32),
        ),
        in_specs=[cube, cube, stripe(rank), fixed(rank, cols)],
        out_specs=(cube, stripe(cols), fixed(rank, cols)),
        scratch_shapes=[pltpu.VMEM((rank, cols), bf16), pltpu.VMEM((3 * rank, cols), bf16)],
        compiler_params=params(), name="finish",
    )(momentum, gradient, orthonormal, factor)
    own = cols // shard_n
    new_factor = lax.dynamic_slice_in_dim(new, lax.axis_index("fsdp") * own, own, axis=1).T
    return new_momentum, update, new_factor


def by_collectives(reps, shard_n, total_rows, momentum, gradient, right_factor):
    buffer = momentum[0] + gradient[0].astype(f32)
    partial = exact(buffer, lax.all_gather(right_factor, "fsdp", axis=0, tiled=True))
    projected = lax.psum(partial, "rep")
    gram_matrix = lax.psum(exact(projected, projected, TN), "fsdp")
    lower_factor = jnp.linalg.cholesky(gram_matrix)
    orthonormal = jax.scipy.linalg.solve_triangular(lower_factor, projected.T, lower=True).T
    scattered = lax.psum_scatter(
        exact(buffer, orthonormal, TN), "fsdp", scatter_dimension=0, tiled=True)
    own_factor = lax.psum(scattered, "rep") / reps
    full_factor = lax.all_gather(own_factor, "fsdp", axis=0, tiled=True)
    col_norms = jnp.sqrt(jnp.sum(full_factor * full_factor, axis=0) + epsilon)
    new_factor = own_factor / col_norms
    correction = exact(orthonormal, full_factor, NT)
    new_momentum = (buffer - (1.0 - decay_rate) * correction)[None]
    direction = exact(orthonormal, full_factor / col_norms, NT)
    scale = math.sqrt(total_rows * buffer.shape[1] / right_factor.shape[1])
    return new_momentum, (scale * direction).astype(bf16), new_factor


def solution(mesh):
    reps, shard_n = mesh.shape["rep"], mesh.shape["fsdp"]

    def shards(momentum, gradient, right_factor):
        rows, cols = momentum.shape[1:]
        rank = right_factor.shape[1]
        fits = (
            reps == 4 and shard_n % 2 == 0 and shard_n > 2 and rows % 128 == 0
            and (cols // shard_n) % 8 == 0 and cols % 256 == 0
            and rank % (8 * reps * shard_n) == 0
        )
        run = by_kernels if fits else by_collectives
        return run(reps, shard_n, rows * shard_n, momentum, gradient, right_factor)

    in_specs = (P("rep", "fsdp", None), P("rep", "fsdp", None), P("fsdp", None))
    out_specs = (P("rep", "fsdp", None), P("fsdp", None), P("fsdp", None))
    return jax.shard_map(shards, mesh=mesh, in_specs=in_specs, out_specs=out_specs, check_vma=False)
```

profile of v0, /device:TPU:1, one launch (start us, length us, event | category | flops | bytes accessed | tf_op | source)
XLA Modules:
  0.0 222.6 jit_solution(7768278734845446633)
XLA Ops:
  0.6 29.6 %gather_right.1.right_ref = f32[2304,256]{1,0:T(8,128)} custom-call(f32[288,256]{1,0:T(8,128)} %own_ref.1), custom_call_target="tpu_custom_call" | custom-call | tf_op jit(solution)/shard_map/gather_right/pallas_call | solution.py:373
  30.3 17.9 %project.1.part_ref = f32[2304,256]{1,0:T(8,128)} custom-call(f32[1,2304,2304]{2,1,0:T(8,128)} %m_ref.5, bf16[1,2304,2304]{2,1,0:T(8,128)(2,1)} %g_ref.5, f32[2304,256]{1,0:T(8,128)} %gather_right.1.right_ref), custom_call_target="tpu_custom_call" | custom-call | tf_op jit(solution)/shard_map/project/pallas_call | solution.py:381
  48.2 82.3 %orthonormalize.1.q_ref = f32[2304,256]{1,0:T(8,128)} custom-call(f32[2304,256]{1,0:T(8,128)} %project.1.part_ref), custom_call_target="tpu_custom_call" | custom-call | tf_op jit(solution)/shard_map/orthonormalize/pallas_call | solution.py:390
  130.4 18.6 %factor_term.1.part_ref = f32[256,2304]{1,0:T(8,128)} custom-call(f32[1,2304,2304]{2,1,0:T(8,128)} %m_ref.5, bf16[1,2304,2304]{2,1,0:T(8,128)(2,1)} %g_ref.5, f32[2304,256]{1,0:T(8,128)} %orthonormalize.1.q_ref), custom_call_target="tpu_custom_call" | custom-call | tf_op jit(solution)/shard_map/factor_term/pallas_call | solution.py:406
  149.0 43.9 %sum_factor.1.factor_ref = f32[256,2304]{1,0:T(8,128)} custom-call(f32[256,2304]{1,0:T(8,128)} %factor_term.1.part_ref), custom_call_target="tpu_custom_call" | custom-call | tf_op jit(solution)/shard_map/sum_factor/pallas_call | solution.py:414
  192.9 27.6 %finish.1 = (f32[1,2304,2304]{2,1,0:T(8,128)}, bf16[2304,2304]{1,0:T(8,128)(2,1)}, f32[256,2304]{1,0:T(8,128)}) custom-call(f32[1,2304,2304]{2,1,0:T(8,128)} %m_ref.5, bf16[1,2304,2304]{2,1,0:T(8,128)(2,1)} %g_ref.5, f32[2304,256]{1,0:T(8,128)} %orthonormalize.1.q_ref, f32[256,2304]{1,0:T(8,128)} %sum_factor.1.factor_ref), custom_call_target="tpu_custom_call" | custom-call | tf_op jit(solution)/shard_map/finish/pallas_call | solution.py:428
  220.5 1.2 dynamic-slice_bitcast_fusion
  221.7 0.9 copy.6
where the time goes:
time: 224 us; the launch traced here: 223 us
  Pallas kernels  220 us (98%)
    pallas_call x1, Pallas kernels, by_kernels(): pl.pallas_call(functools.partial(orthonormalize, reps, shard_n), out_shap...  82.3 us
    pallas_call x1, Pallas kernels, by_kernels(): pl.pallas_call(functools.partial(sum_factor, reps, shard_n), out_shape=ja...  43.9 us
    pallas_call x1, Pallas kernels, by_kernels(): pl.pallas_call(functools.partial(gather_right, shard_n), out_shape=jax.Sh...  29.6 us
    pallas_call x1, Pallas kernels, by_kernels(): pl.pallas_call(functools.partial(finish, math.sqrt(total_rows * cols / ra...  27.6 us
    pallas_call x1, Pallas kernels, by_kernels(): pl.pallas_call(factor_term, grid=(steps,), out_shape=jax.ShapeDtypeStruct...  18.6 us
    pallas_call x1, Pallas kernels, by_kernels(): pl.pallas_call(project, grid=(steps,), out_shape=jax.ShapeDtypeStruct((ro...  17.9 us

commit v1 on v0

v1 whole, which is shorter than its diff:
```python
import functools
import math

import jax
import jax.numpy as jnp
from jax import lax
from jax.experimental import pallas as pl
from jax.experimental.pallas import tpu as pltpu
from jax.sharding import PartitionSpec as P

epsilon = 1e-06
decay_rate = 0.95
highest = lax.Precision.HIGHEST
f32 = jnp.float32
bf16 = jnp.bfloat16
MESH = pl.DeviceIdType.MESH


def split(x):
    high = x.astype(bf16)
    return high, (x - high.astype(f32)).astype(bf16)


def dot(a, b, dims=(((1,), (0,)), ((), ()))):
    return lax.dot_general(a, b, dims, preferred_element_type=f32)


def exact(a, b, dims=(((1,), (0,)), ((), ()))):
    return lax.dot_general(a, b, dims, precision=highest, preferred_element_type=f32)


NT = (((1,), (1,)), ((), ()))
TN = (((0,), (0,)), ((), ()))


def greet(peers):
    barrier = pltpu.get_barrier_semaphore()
    for peer in peers:
        pl.semaphore_signal(barrier, inc=1, device_id=peer, device_id_type=MESH)
    pl.semaphore_wait(barrier, len(peers))


def remote(src, dst, send_sem, recv_sem, peer):
    copy = pltpu.make_async_remote_copy(
        src_ref=src, dst_ref=dst, send_sem=send_sem, recv_sem=recv_sem,
        device_id=peer, device_id_type=MESH,
    )
    copy.start()
    return copy


def product(a, b, dims=(((1,), (0,)), ((), ()))):
    ah, al = split(a)
    bh, bl = split(b)
    return dot(ah, bh, dims) + dot(ah, bl, dims) + dot(al, bh, dims)


def inverse_small(a, size):
    row = lax.broadcasted_iota(jnp.int32, (size, 2 * size), 0)
    lane = lax.broadcasted_iota(jnp.int32, (size, 2 * size), 1)
    eye = jnp.where(row == lane - size, 1.0, 0.0).astype(f32)
    work = jnp.concatenate([a, eye[:, size:]], axis=1)
    for j in range(size):
        first = (j // 8) * 8
        pivot = work[j:j + 1, :]
        scaled = pivot / work[j:j + 1, j:j + 1]
        tail = work[first:, :]
        below = row[first:, :] > j
        tail = tail - jnp.where(below, tail[:, j:j + 1], 0.0) * scaled
        work = tail if first == 0 else jnp.concatenate([work[:first], tail], axis=0)
    diag = jnp.sum(jnp.where(row == lane, work, 0.0), axis=1, keepdims=True)
    return work[:, size:] * (1.0 / jnp.sqrt(diag))


def inverse_lower(a, size):
    if size <= 64:
        result = inverse_small(a, size)
        yield
        return result
    h = size // 2
    top = yield from inverse_lower(a[:h, :h], h)
    cross = exact(a[h:, :h], top, NT)
    low = yield from inverse_lower(a[h:, h:] - exact(cross, cross, NT), h)
    corner = -exact(low, exact(cross, top))
    return jnp.concatenate(
        [jnp.concatenate([top, jnp.zeros((h, h), f32)], axis=1),
         jnp.concatenate([corner, low], axis=1)], axis=0)


def reduce_all(
    reps, shard_n, tile, m_ref, g_ref, own_ref, bh, bl, qh, ql, wsum, inv,
    ms, gs, rfull, rh, rl, part, full, pt, wacc,
    xin, yin, xin2, yin2, gout, gin, gz, gfull, cin, wx, wy, wx2, wy2, zin, zsum,
    lsem, own_sem, rsend, rrecv, send, recv, gsend, grecv, csend, crecv,
):
    r = lax.axis_index("rep")
    f = lax.axis_index("fsdp")
    rows, cols = bh.shape
    own_rows, rank = own_ref.shape
    chips = shard_n // 2
    chip, core = f // 2, lax.rem(f, 2)
    half = rank // 2
    chunk = rows // reps
    sx = 1 - 2 * lax.rem(r, 2)
    sy = 1 - 2 * (r // 2)
    px, py, pd = r + sx, r + 2 * sy, r + sx + 2 * sy
    at_x, at_y, mate = (px, f), (py, f), (r, chip * 2 + 1 - core)
    left, right = pl.ds(0, half), pl.ds(half, half)
    tiles, slots = rows // tile, ms.shape[0]
    total = reps * shard_n
    me = r * shard_n + f

    def load(t):
        at, slot = pl.ds(t * tile, tile), t % slots
        return (pltpu.make_async_copy(m_ref.at[0, at], ms.at[slot], lsem.at[0, slot]),
                pltpu.make_async_copy(g_ref.at[0, at], gs.at[slot], lsem.at[1, slot]))

    for t in range(slots):
        for copy in load(t):
            copy.start()

    others = [lax.rem(me + k, total) for k in range(1, total)]
    greet([(d // shard_n, lax.rem(d, shard_n)) for d in others])

    def block(index):
        return pl.ds(pl.multiple_of(index * own_rows, 8), own_rows)

    quarter = own_rows // reps

    def part_of(index, rep):
        return pl.ds(pl.multiple_of(index * own_rows + rep * quarter, 8), quarter)

    def rsend_to(src, dst, k, peer):
        return remote(src, dst, rsend.at[k], rrecv.at[k], peer)

    local = pltpu.make_async_copy(own_ref, rfull.at[block(f)], own_sem)
    local.start()
    gz1 = [rsend_to(own_ref.at[pl.ds(pl.multiple_of(r * quarter, 8), quarter)], rfull.at[part_of(f, r)], k,
                    (r, lax.rem(chip + k + 1, chips) * 2 + core)) for k in range(chips - 1)]
    mates = [rsend_to(own_ref, rfull.at[block(f)], chips, mate)]
    source = [lax.rem(chip + chips - k - 1, chips) * 2 + core for k in range(chips - 1)]
    ax, ay, fx, fy = {}, {}, {}, {}

    def spread(k):
        gz1[k].wait_recv()
        mine = rfull.at[part_of(source[k], r)]
        ax[k] = rsend_to(mine, mine, (2 * chips) + k, at_x)
        ay[k] = rsend_to(mine, mine, (3 * chips) + k, at_y)

    def forward(k):
        ax[k].wait_recv()
        piece = rfull.at[part_of(source[k], px), left]
        fx[k] = rsend_to(piece, piece, (4 * chips) + k, at_y)
        ay[k].wait_recv()
        piece = rfull.at[part_of(source[k], py), right]
        fy[k] = rsend_to(piece, piece, (5 * chips) + k, at_x)

    def pass_on(k):
        fx[k].wait_recv()
        fy[k].wait_recv()
        piece = rfull.at[block(source[k])]
        mates.append(rsend_to(piece, piece, chips + k + 1, mate))

    actions = [functools.partial(spread, k) for k in range(chips - 1)]
    actions += [functools.partial(forward, k) for k in range(chips - 1)]
    begin = tiles // 4
    places = [begin + (i * (tiles - begin)) // len(actions) for i in range(len(actions))]
    sub = 32 if tile % 32 == 0 else 16
    for t in range(tiles):
        slot = t % slots
        for copy in load(t):
            copy.wait()

        @pl.loop(0, tile // sub)
        def _(i):
            src = pl.ds(pl.multiple_of(i * sub, sub), sub)
            dst = pl.ds(pl.multiple_of(t * tile + i * sub, sub), sub)
            bh[dst, :], bl[dst, :] = split(ms[slot, src, :] + gs[slot, src, :].astype(f32))

        if t + slots < tiles:
            for copy in load(t + slots):
                copy.start()
        for i, action in enumerate(actions):
            if places[i] == t:
                action()
    for k in range(chips - 1):
        pass_on(k)
    local.wait()
    for copy in mates:
        copy.wait_recv()

    @pl.loop(0, shard_n)
    def _(i):
        at = pl.ds(pl.multiple_of(i * own_rows, 16), own_rows)
        rh[at, :], rl[at, :] = split(rfull[at, :])

    def of(index):
        return pl.ds(pl.multiple_of(index * chunk, 16), chunk)

    def project(which):
        step = chunk // 2

        @pl.loop(0, 2)
        def _(i):
            at = pl.ds(pl.multiple_of(which * chunk + i * step, 16), step)
            high = bh[at, :]
            part[at, :] = dot(high, rh[...]) + dot(high, rl[...]) + dot(bl[at, :], rh[...])

    def exchange(src, dst, k, peer):
        return remote(src, dst, send.at[k], recv.at[k], peer)

    project(pd)
    s1 = [exchange(part.at[of(pd), left], xin.at[0], 0, at_x),
          exchange(part.at[of(pd), right], yin.at[0], 1, at_y)]
    project(px)
    s1.append(exchange(part.at[of(px), left], xin.at[1], 2, at_x))
    project(py)
    s1.append(exchange(part.at[of(py), right], yin.at[1], 3, at_y))
    s1[0].wait_recv()
    xin[0] = xin[0] + part[of(py), left]
    a = exchange(xin.at[0], xin2, 4, at_y)
    s1[1].wait_recv()
    yin[0] = yin[0] + part[of(px), right]
    b = exchange(yin.at[0], yin2, 5, at_x)
    project(r)
    s1[2].wait_recv()
    xin[1] = xin[1] + part[of(r), left]
    s1[3].wait_recv()
    yin[1] = yin[1] + part[of(r), right]
    a.wait_recv()
    full[of(r), left] = xin[1] + xin2[...]
    b.wait_recv()
    full[of(r), right] = yin[1] + yin2[...]
    whole = of(r)
    t1 = [
        exchange(full.at[whole, left], full.at[whole, left], 6, at_x),
        exchange(full.at[whole, right], full.at[whole, right], 7, at_y),
        exchange(full.at[whole, right], full.at[whole, right], 8, at_x),
        exchange(full.at[whole, left], full.at[whole, left], 9, at_y),
    ]

    own = full[whole, :]
    gout[...] = exact(own, own, TN)
    piece = rank // shard_n

    def rows_of(index):
        return pl.ds(pl.multiple_of(index * piece, 8), piece)

    def gram_to(src, dst, k, peer):
        return remote(src, dst, gsend.at[k], grecv.at[k], peer)

    peers = [lax.rem(f + k, shard_n) for k in range(1, shard_n)]
    g1 = [gram_to(gout.at[rows_of(d)], gin.at[k], k, (r, d)) for k, d in enumerate(peers)]

    def left_factor(which, first):
        at = of(which)
        high, low = split(full[at, :].T)
        pt[...] = jnp.concatenate([high, low], axis=0)
        wide = 768 if cols % 768 == 0 else 256

        @pl.loop(0, cols // wide)
        def _(i):
            to = pl.ds(pl.multiple_of(i * wide, 128), wide)
            both = dot(pt[...], bh[at, to])
            term = both[:rank] + both[rank:] + dot(pt[:rank, :], bl[at, to])
            wacc[:, to] = term if first else wacc[:, to] + term

    left_factor(r, True)
    acc = gout[rows_of(f), :]
    for k in range(shard_n - 1):
        g1[k].wait_recv()
        acc = acc + gin[k]
    gz[0] = acc
    g2 = [gram_to(gz.at[0], gz.at[k + 1], shard_n + k, peer) for k, peer in enumerate((at_x, at_y, (pd, f)))]
    t1[0].wait_recv()
    t2 = [exchange(full.at[of(px), left], full.at[of(px), left], 10, at_y)]
    t1[1].wait_recv()
    t2.append(exchange(full.at[of(py), right], full.at[of(py), right], 11, at_x))
    t1[2].wait_recv()
    left_factor(px, False)
    for copy in g2:
        copy.wait_recv()
    gfull[rows_of(f), :] = (gz[0] + gz[1]) + (gz[2] + gz[3])
    mine = gfull.at[rows_of(f)]
    g3 = [gram_to(mine, mine, shard_n + 4 + k, (r, d)) for k, d in enumerate(peers)]
    t1[3].wait_recv()
    left_factor(py, False)
    t2[0].wait_recv()
    t2[1].wait_recv()
    left_factor(pd, False)

    n0 = rank // 2
    n1 = n0 // reps
    n2 = n1 // chips
    wide = cols // 2
    lo, hi = pl.ds(0, wide), pl.ds(wide, wide)
    zs = [lax.rem(chip + k, chips) for k in range(1, chips)]

    def group_of(index):
        return pl.ds(pl.multiple_of(index * n1, 8), n1)

    def factor_to(src, dst, k, peer):
        return remote(src, dst, csend.at[k], crecv.at[k], peer)

    base = core * n0
    c = []
    for k, which in enumerate([pd, px, py, r]):
        away = pl.ds(pl.multiple_of((1 - core) * n0 + which * n1, 8), n1)
        c.append(factor_to(wacc.at[away], cin.at[group_of(which)], k, mate))

    def add_own(which):
        at = pl.ds(pl.multiple_of(base + which * n1, 8), n1)
        cin[group_of(which), :] = cin[group_of(which), :] + wacc[at, :]

    def invert():
        inv[...] = yield from inverse_lower(gfull[...], rank)
        yield

    steps = invert()
    c[0].wait_recv()
    add_own(pd)
    w1 = [factor_to(cin.at[group_of(pd), lo], wx.at[0], 4, at_x),
          factor_to(cin.at[group_of(pd), hi], wy.at[0], 5, at_y)]
    c[1].wait_recv()
    add_own(px)
    w1.append(factor_to(cin.at[group_of(px), lo], wx.at[1], 6, at_x))
    c[2].wait_recv()
    add_own(py)
    w1.append(factor_to(cin.at[group_of(py), hi], wy.at[1], 7, at_y))
    c[3].wait_recv()
    add_own(r)
    for copy in g3:
        copy.wait_recv()
    w1[0].wait_recv()
    wx[0] = wx[0] + cin[group_of(py), lo]
    wa = factor_to(wx.at[0], wx2, 8, at_y)
    w1[1].wait_recv()
    wy[0] = wy[0] + cin[group_of(px), hi]
    wb = factor_to(wy.at[0], wy2, 9, at_x)
    next(steps)
    w1[2].wait_recv()
    wx[1] = wx[1] + cin[group_of(r), lo]
    w1[3].wait_recv()
    wy[1] = wy[1] + cin[group_of(r), hi]
    wa.wait_recv()
    zsum[:, lo] = wx[1] + wx2[...]
    wb.wait_recv()
    zsum[:, hi] = wy[1] + wy2[...]
    z1 = []
    for k, z in enumerate(zs):
        at = pl.ds(pl.multiple_of(z * n2, 8), n2)
        z1.append(factor_to(zsum.at[at], zin.at[k], 20 + k, (r, z * 2 + core)))
    next(steps)
    acc = zsum[pl.ds(pl.multiple_of(chip * n2, 8), n2), :]
    for k in range(chips - 1):
        z1[k].wait_recv()
        acc = acc + zin[k]

    def group(rep):
        return pl.ds(pl.multiple_of(base + rep * n1, 8), n1)

    at = pl.ds(pl.multiple_of(base + r * n1 + chip * n2, 8), n2)
    wsum[at, :] = acc * (1.0 / reps)
    z2 = [factor_to(wsum.at[at], wsum.at[at], 20 + chips + k, (r, z * 2 + core)) for k, z in enumerate(zs)]
    next(steps)
    for copy in z2:
        copy.wait_recv()
    gr, gx, gy, gd = group(r), group(px), group(py), group(pd)

    def share(at, k, peer):
        return factor_to(wsum.at[at], wsum.at[at], k, peer)

    t = [share((gr, lo), 10, at_x), share((gr, hi), 11, at_y), share((gr, hi), 12, at_x),
         share((gr, lo), 13, at_y), share((gr,), 14, mate)]
    next(steps)
    t[0].wait_recv()
    t.append(share((gx, lo), 15, at_y))
    t[1].wait_recv()
    t.append(share((gy, hi), 16, at_x))
    next(steps)

    step = 256 if rows % 256 == 0 else chunk

    @pl.loop(0, rows // step)
    def _(i):
        at = pl.ds(pl.multiple_of(i * step, 16), step)
        qh[at, :], ql[at, :] = split(product(full[at, :], inv[...], NT))

    t[2].wait_recv()
    t.append(share((gx,), 17, mate))
    t[3].wait_recv()
    t.append(share((gy,), 18, mate))
    t[5].wait_recv()
    t[6].wait_recv()
    t.append(share((gd,), 19, mate))
    for index in (4, 7, 8, 9):
        t[index].wait_recv()
    sent = gz1 + mates + s1 + [a, b] + t1 + t2 + g1 + g2 + g3 + c + w1 + [wa, wb] + z1 + z2 + t
    for copies in (ax, ay, fx, fy):
        sent += [copies[k] for k in range(chips - 1)]
    for copy in sent:
        copy.wait_send()


def finish(scale, shard_n, bh, bl, qh, ql, w_ref, inv, mom_ref, upd_ref, new_ref, plain, high, low, norm):
    i = pl.program_id(0)

    @pl.when(i == 0)
    def _():
        rank, cols = plain.shape
        factor = product(inv[...], w_ref[...])
        norms = jnp.sqrt(jnp.sum(factor * factor, axis=1, keepdims=True) + epsilon)
        new = factor / norms
        norm[...] = new
        plain[...] = ((1.0 - decay_rate) * factor).astype(bf16)
        high[...], low[...] = split(new)
        f = lax.axis_index("fsdp")
        own = cols // shard_n
        span = new_ref.shape[0] + 128 - math.gcd(own, 128)
        first = (f * own) // 128
        window = norm[:, pl.ds(pl.multiple_of(first * 128, 128), span)]
        window = pltpu.roll(window, lax.rem(span - (f * own - first * 128), span), 1)
        new_ref[...] = window[:, :own].T

    tile = upd_ref.shape[0]
    at = pl.ds(pl.multiple_of(i * tile, tile), tile)
    q1, q2 = qh[at, :], ql[at, :]
    mom_ref[0] = (bh[at, :].astype(f32) + bl[at, :].astype(f32)) - dot(q1, plain[...])
    direction = dot(q1, high[...]) + dot(q1, low[...]) + dot(q2, high[...])
    upd_ref[...] = (scale * direction).astype(bf16)


def params(limit, **more):
    return pltpu.CompilerParams(vmem_limit_bytes=limit * 1024 * 1024, **more)


def by_kernels(reps, shard_n, total_rows, momentum, gradient, right_factor):
    _, rows, cols = momentum.shape
    own_rows, rank = right_factor.shape
    vmem = pl.BlockSpec(memory_space=pltpu.VMEM)
    dma = pltpu.SemaphoreType.DMA
    chips = shard_n // 2
    chunk, half = rows // reps, rank // 2
    n1 = rank // 2 // reps
    tile = rows // 12
    vm = pltpu.VMEM
    kept = [vm((rows, cols), bf16), vm((rows, cols), bf16), vm((rows, rank), bf16), vm((rows, rank), bf16),
            vm((rank, cols), f32), vm((rank, rank), f32)]
    kept = pl.pallas_call(
        functools.partial(reduce_all, reps, shard_n, tile),
        out_shape=kept,
        in_specs=[pl.BlockSpec(memory_space=pl.ANY)] * 2 + [vmem], out_specs=[vmem] * 6,
        scratch_shapes=[
            vm((3, tile, cols), f32), vm((3, tile, cols), bf16),
            vm((cols, rank), f32), vm((cols, rank), bf16), vm((cols, rank), bf16),
            vm((rows, rank), f32), vm((rows, rank), f32), vm((2 * rank, chunk), bf16), vm((rank, cols), f32),
            vm((2, chunk, half), f32), vm((2, chunk, half), f32), vm((chunk, half), f32), vm((chunk, half), f32),
            vm((rank, rank), f32), vm((shard_n - 1, rank // shard_n, rank), f32),
            vm((4, rank // shard_n, rank), f32), vm((rank, rank), f32),
            vm((half, cols), f32), vm((2, n1, cols // 2), f32), vm((2, n1, cols // 2), f32),
            vm((n1, cols // 2), f32), vm((n1, cols // 2), f32),
            vm((chips - 1, n1 // chips, cols), f32), vm((n1, cols), f32),
            dma((2, 3)), dma, dma((6 * chips,)), dma((6 * chips,)), dma((12,)), dma((12,)),
            dma((2 * shard_n + 4,)), dma((2 * shard_n + 4,)), dma((20 + 2 * chips,)), dma((20 + 2 * chips,)),
        ],
        compiler_params=params(35, collective_id=0, has_side_effects=True),
        name="reduce_all",
    )(momentum, gradient, right_factor)
    step = 256 if rows % 256 == 0 else rows // 8
    return pl.pallas_call(
        functools.partial(finish, math.sqrt(total_rows * cols / rank), shard_n),
        grid=(rows // step,),
        out_shape=(
            jax.ShapeDtypeStruct(momentum.shape, f32),
            jax.ShapeDtypeStruct((rows, cols), bf16),
            jax.ShapeDtypeStruct((cols // shard_n, rank), f32),
        ),
        in_specs=[vmem] * 6,
        out_specs=(pl.BlockSpec((1, step, cols), lambda i: (0, i, 0)), pl.BlockSpec((step, cols), lambda i: (i, 0)),
                   pl.BlockSpec((cols // shard_n, rank), lambda i: (0, 0))),
        scratch_shapes=[vm((rank, cols), bf16)] * 3 + [vm((rank, cols), f32)],
        compiler_params=params(35), name="finish",
    )(*[pltpu.with_memory_space_constraint(x, pltpu.VMEM) for x in kept])


def by_collectives(reps, shard_n, total_rows, momentum, gradient, right_factor):
    buffer = momentum[0] + gradient[0].astype(f32)
    partial = exact(buffer, lax.all_gather(right_factor, "fsdp", axis=0, tiled=True))
    projected = lax.psum(partial, "rep")
    gram_matrix = lax.psum(exact(projected, projected, TN), "fsdp")
    lower_factor = jnp.linalg.cholesky(gram_matrix)
    orthonormal = jax.scipy.linalg.solve_triangular(lower_factor, projected.T, lower=True).T
    scattered = lax.psum_scatter(
        exact(buffer, orthonormal, TN), "fsdp", scatter_dimension=0, tiled=True)
    own_factor = lax.psum(scattered, "rep") / reps
    full_factor = lax.all_gather(own_factor, "fsdp", axis=0, tiled=True)
    col_norms = jnp.sqrt(jnp.sum(full_factor * full_factor, axis=0) + epsilon)
    new_factor = own_factor / col_norms
    correction = exact(orthonormal, full_factor, NT)
    new_momentum = (buffer - (1.0 - decay_rate) * correction)[None]
    direction = exact(orthonormal, full_factor / col_norms, NT)
    scale = math.sqrt(total_rows * buffer.shape[1] / right_factor.shape[1])
    return new_momentum, (scale * direction).astype(bf16), new_factor


def solution(mesh):
    reps, shard_n = mesh.shape["rep"], mesh.shape["fsdp"]

    def shards(momentum, gradient, right_factor):
        rows, cols = momentum.shape[1:]
        rank = right_factor.shape[1]
        fits = (
            reps == 4 and shard_n % 2 == 0 and shard_n > 2 and rows % 1152 == 0
            and (cols // shard_n) % 96 == 0 and cols % 256 == 0
            and rank % (8 * reps * shard_n) == 0
        )
        run = by_kernels if fits else by_collectives
        return run(reps, shard_n, rows * shard_n, momentum, gradient, right_factor)

    in_specs = (P("rep", "fsdp", None), P("rep", "fsdp", None), P("fsdp", None))
    out_specs = (P("rep", "fsdp", None), P("fsdp", None), P("fsdp", None))
    return jax.shard_map(shards, mesh=mesh, in_specs=in_specs, out_specs=out_specs, check_vma=False)
```

time: 224 us -> 149 us (0.67)
  Pallas kernels: 220 us -> 148 us
    pallas_call x5 -> x1, Pallas kernels: 192 us -> 131 us  [by_kernels(): pl.pallas_call(functools.partial(reduce_all, reps, shard_n, tile), out_sh...]
    pallas_call x1, Pallas kernels: 27.6 us -> 16.4 us  [by_kernels(): pl.pallas_call(functools.partial(finish, math.sqrt(total_rows * cols / ra...]
where the time goes in v1:
time: 149 us
  Pallas kernels  148 us (99%)
    pallas_call x1, Pallas kernels, by_kernels(): pl.pallas_call(functools.partial(reduce_all, reps, shard_n, tile), out_sh...  131 us
    pallas_call x1, Pallas kernels, by_kernels(): pl.pallas_call(functools.partial(finish, math.sqrt(total_rows * cols / ra...  16.4 us

profile of v1, /device:TPU:1, one launch (start us, length us, event | category | flops | bytes accessed | tf_op | source)
XLA Modules:
  0.0 148.5 jit_solution(15534988945192083817)
XLA Ops:
  0.6 131.5 %reduce_all.1 = (bf16[2304,2304]{1,0:T(8,128)(2,1)S(1)}, bf16[2304,2304]{1,0:T(8,128)(2,1)S(1)}, bf16[2304,256]{1,0:T(8,128)(2,1)S(1)}, bf16[2304,256]{1,0:T(8,1...) custom-call(f32[1,2304,2304]{2,1,0:T(8,128)} %m_ref.1, bf16[1,2304,2304]{2,1,0:T(8,128)(2,1)} %g_ref.1, ...), custom_call_target="tpu_custom_call" | custom-call | tf_op jit(solution)/shard_map/reduce_all/pallas_call | solution.py:449
  132.1 16.4 %finish.1 = (f32[1,2304,2304]{2,1,0:T(8,128)}, bf16[2304,2304]{1,0:T(8,128)(2,1)}, f32[288,256]{1,0:T(8,128)}) custom-call(bf16[2304,2304]{1,0:T(8,128)(2,1)S(1)} %get-tuple-element.9.bh, bf16[2304,2304]{1,0:T(8,128)(2,1)S(1)} %get-tuple-element.10.bl, bf16[2304,256]{1,0:T(8,128)(2,1)S(1)} %get-tuple-element.11.qh, ...), custom_call_target="tpu_custom_call" | custom-call | tf_op jit(solution)/shard_map/finish/pallas_call | solution.py:470

commit v2 on v1

--- a/solution.py
+++ b/solution.py
@@ -1,4 +1,5 @@
 import functools
+import itertools
 import math
 
 import jax
@@ -14,6 +15,7 @@
 f32 = jnp.float32
 bf16 = jnp.bfloat16
 MESH = pl.DeviceIdType.MESH
+ORDER = ("LaLbabLcLdacdbiiaiciiidiiabicid", "iiiaiibiiaicaiiqadbacbbdccbdbdcdcd")
 
 
 def split(x):
@@ -56,27 +58,37 @@
 
 
 def inverse_small(a, size):
-    row = lax.broadcasted_iota(jnp.int32, (size, 2 * size), 0)
-    lane = lax.broadcasted_iota(jnp.int32, (size, 2 * size), 1)
+    wide = 2 * size
+    row = lax.broadcasted_iota(jnp.int32, (size, wide), 0)
+    lane = lax.broadcasted_iota(jnp.int32, (size, wide), 1)
     eye = jnp.where(row == lane - size, 1.0, 0.0).astype(f32)
     work = jnp.concatenate([a, eye[:, size:]], axis=1)
-    for j in range(size):
-        first = (j // 8) * 8
-        pivot = work[j:j + 1, :]
-        scaled = pivot / work[j:j + 1, j:j + 1]
-        tail = work[first:, :]
-        below = row[first:, :] > j
-        tail = tail - jnp.where(below, tail[:, j:j + 1], 0.0) * scaled
-        work = tail if first == 0 else jnp.concatenate([work[:first], tail], axis=0)
+    for j in range(0, size, 8):
+        tail = work[j:, :]
+        ends = range(j, j + 8)
+        pivots = [work[i:i + 1, :] for i in ends]
+        corner = [[jnp.broadcast_to(work[i:i + 1, k:k + 1], (1, wide)) for k in ends] for i in ends]
+        columns = [jnp.broadcast_to(tail[:, i:i + 1], tail.shape) for i in ends]
+        for i in range(8):
+            inverse = 1.0 / corner[i][i]
+            for k in range(i + 1, 8):
+                ratio = corner[i][k] * inverse
+                pivots[k] = pivots[k] - ratio * pivots[i]
+                columns[k] = columns[k] - ratio * columns[i]
+                for m in range(k, 8):
+                    corner[k][m] = corner[k][m] - ratio * corner[i][m]
+            below = row[j:, :] > j + i
+            tail = tail - jnp.where(below, columns[i], 0.0) * (pivots[i] * inverse)
+        work = tail if j == 0 else jnp.concatenate([work[:j], tail], axis=0)
+        if j % 16 == 8:
+            yield
     diag = jnp.sum(jnp.where(row == lane, work, 0.0), axis=1, keepdims=True)
     return work[:, size:] * (1.0 / jnp.sqrt(diag))
 
 
 def inverse_lower(a, size):
     if size <= 64:
-        result = inverse_small(a, size)
-        yield
-        return result
+        return (yield from inverse_small(a, size))
     h = size // 2
     top = yield from inverse_lower(a[:h, :h], h)
     cross = exact(a[h:, :h], top, NT)
@@ -88,9 +100,9 @@
 
 
 def reduce_all(
-    reps, shard_n, tile, m_ref, g_ref, own_ref, bh, bl, qh, ql, wsum, inv,
+    reps, shard_n, tile, widths, m_ref, g_ref, own_ref, bh, bl, q, fh, fl, norm, wsum, inv,
     ms, gs, rfull, rh, rl, part, full, pt, wacc,
-    xin, yin, xin2, yin2, gout, gin, gz, gfull, cin, wx, wy, wx2, wy2, zin, zsum,
+    xin, yin, xin2, yin2, gout, gin, gz, gfull, cin, wx, wy, zin, zsum,
     lsem, own_sem, rsend, rrecv, send, recv, gsend, grecv, csend, crecv,
 ):
     r = lax.axis_index("rep")
@@ -107,8 +119,6 @@
     at_x, at_y, mate = (px, f), (py, f), (r, chip * 2 + 1 - core)
     left, right = pl.ds(0, half), pl.ds(half, half)
     tiles, slots = rows // tile, ms.shape[0]
-    total = reps * shard_n
-    me = r * shard_n + f
 
     def load(t):
         at, slot = pl.ds(t * tile, tile), t % slots
@@ -119,8 +129,7 @@
         for copy in load(t):
             copy.start()
 
-    others = [lax.rem(me + k, total) for k in range(1, total)]
-    greet([(d // shard_n, lax.rem(d, shard_n)) for d in others])
+    greet([at_x, at_y, (pd, f)] + [(r, lax.rem(f + k, shard_n)) for k in range(1, shard_n)])
 
     def block(index):
         return pl.ds(pl.multiple_of(index * own_rows, 8), own_rows)
@@ -183,42 +192,57 @@
         for i, action in enumerate(actions):
             if places[i] == t:
                 action()
+    def split_rows(index):
+        at = pl.ds(pl.multiple_of(index * own_rows, 16), own_rows)
+        rh[at, :], rl[at, :] = split(rfull[at, :])
+
+    local.wait()
+    split_rows(f)
+    mates[0].wait_recv()
+    split_rows(chip * 2 + 1 - core)
     for k in range(chips - 1):
         pass_on(k)
-    local.wait()
-    for copy in mates:
-        copy.wait_recv()
-
-    @pl.loop(0, shard_n)
-    def _(i):
-        at = pl.ds(pl.multiple_of(i * own_rows, 16), own_rows)
-        rh[at, :], rl[at, :] = split(rfull[at, :])
+        split_rows(source[k])
+    for k in range(chips - 1):
+        mates[k + 1].wait_recv()
+        split_rows(lax.rem(chip + chips - k - 1, chips) * 2 + 1 - core)
 
     def of(index):
         return pl.ds(pl.multiple_of(index * chunk, 16), chunk)
 
+    half_rows = chunk // 2
+
+    def half_of(which, i):
+        return pl.ds(pl.multiple_of(which * chunk + i * half_rows, 16), half_rows)
+
+    def project_half(which, i):
+        at = half_of(which, i)
+        high = bh[at, :]
+        part[at, :] = dot(high, rh[...]) + dot(high, rl[...]) + dot(bl[at, :], rh[...])
+
     def project(which):
-        step = chunk // 2
-
         @pl.loop(0, 2)
         def _(i):
-            at = pl.ds(pl.multiple_of(which * chunk + i * step, 16), step)
-            high = bh[at, :]
-            part[at, :] = dot(high, rh[...]) + dot(high, rl[...]) + dot(bl[at, :], rh[...])
+            project_half(which, i)
 
     def exchange(src, dst, k, peer):
         return remote(src, dst, send.at[k], recv.at[k], peer)
 
-    project(pd)
-    s1 = [exchange(part.at[of(pd), left], xin.at[0], 0, at_x),
-          exchange(part.at[of(pd), right], yin.at[0], 1, at_y)]
+    project_half(pd, 0)
+    early = [exchange(part.at[half_of(pd, 0), left], xin.at[0, :half_rows], 12, at_x),
+             exchange(part.at[half_of(pd, 0), right], yin.at[0, :half_rows], 13, at_y)]
+    project_half(pd, 1)
+    s1 = [exchange(part.at[half_of(pd, 1), left], xin.at[0, half_rows:], 0, at_x),
+          exchange(part.at[half_of(pd, 1), right], yin.at[0, half_rows:], 1, at_y)]
     project(px)
     s1.append(exchange(part.at[of(px), left], xin.at[1], 2, at_x))
     project(py)
     s1.append(exchange(part.at[of(py), right], yin.at[1], 3, at_y))
+    early[0].wait_recv()
     s1[0].wait_recv()
     xin[0] = xin[0] + part[of(py), left]
     a = exchange(xin.at[0], xin2, 4, at_y)
+    early[1].wait_recv()
     s1[1].wait_recv()
     yin[0] = yin[0] + part[of(px), right]
     b = exchange(yin.at[0], yin2, 5, at_x)
@@ -252,18 +276,23 @@
     peers = [lax.rem(f + k, shard_n) for k in range(1, shard_n)]
     g1 = [gram_to(gout.at[rows_of(d)], gin.at[k], k, (r, d)) for k, d in enumerate(peers)]
 
+    def transpose(which):
+        high, low = split(full[of(which), :].T)
+        pt[...] = jnp.concatenate([high, low], axis=0)
+
+    def add_term(which, to, first):
+        at = of(which)
+        both = dot(pt[...], bh[at, to])
+        term = both[:rank] + both[rank:] + dot(pt[:rank, :], bl[at, to])
+        wacc[:, to] = term if first else wacc[:, to] + term
+
     def left_factor(which, first):
-        at = of(which)
-        high, low = split(full[at, :].T)
-        pt[...] = jnp.concatenate([high, low], axis=0)
-        wide = 768 if cols % 768 == 0 else 256
-
-        @pl.loop(0, cols // wide)
+        transpose(which)
+        width = 768 if cols % 768 == 0 else 256
+
+        @pl.loop(0, cols // width)
         def _(i):
-            to = pl.ds(pl.multiple_of(i * wide, 128), wide)
-            both = dot(pt[...], bh[at, to])
-            term = both[:rank] + both[rank:] + dot(pt[:rank, :], bl[at, to])
-            wacc[:, to] = term if first else wacc[:, to] + term
+            add_term(which, pl.ds(pl.multiple_of(i * width, 128), width), first)
 
     left_factor(r, True)
     acc = gout[rows_of(f), :]
@@ -287,147 +316,167 @@
     left_factor(py, False)
     t2[0].wait_recv()
     t2[1].wait_recv()
-    left_factor(pd, False)
-
     n0 = rank // 2
     n1 = n0 // reps
     n2 = n1 // chips
-    wide = cols // 2
-    lo, hi = pl.ds(0, wide), pl.ds(wide, wide)
+    top_rows = n1 // 2
+    streams = len(widths)
+    starts = [sum(widths[:i]) for i in range(streams)]
     zs = [lax.rem(chip + k, chips) for k in range(1, chips)]
-
-    def group_of(index):
-        return pl.ds(pl.multiple_of(index * n1, 8), n1)
-
-    def factor_to(src, dst, k, peer):
-        return remote(src, dst, csend.at[k], crecv.at[k], peer)
-
     base = core * n0
-    c = []
-    for k, which in enumerate([pd, px, py, r]):
-        away = pl.ds(pl.multiple_of((1 - core) * n0 + which * n1, 8), n1)
-        c.append(factor_to(wacc.at[away], cin.at[group_of(which)], k, mate))
-
-    def add_own(which):
-        at = pl.ds(pl.multiple_of(base + which * n1, 8), n1)
-        cin[group_of(which), :] = cin[group_of(which), :] + wacc[at, :]
+    started, squares = [], []
+
+    def factor_sum(index):
+        width = widths[index]
+        at, here = pl.ds(starts[index], width), pl.ds(0, width)
+
+        def of_group(which, start=0, size=n1):
+            return pl.ds(pl.multiple_of(which * n1 + start, 8), size)
+
+        def mine(which, start=0, size=n1):
+            return pl.ds(pl.multiple_of(base + which * n1 + start, 8), size)
+
+        def go(src, dst, k, peer):
+            copy = remote(src, dst, csend.at[index, k], crecv.at[index, k], peer)
+            started.append(copy)
+            return copy
+
+        top, low = (0, top_rows), (top_rows, top_rows)
+        summed, x_in, y_in = cin.at[index, :, here], wx.at[index, :, :, here], wy.at[index, :, :, here]
+        c = []
+        for k, which in enumerate([pd, px, py, r]):
+            away = pl.ds(pl.multiple_of((1 - core) * n0 + which * n1, 8), n1)
+            c.append(go(wacc.at[away, at], summed.at[of_group(which)], k, mate))
+        yield
+
+        def add_own(k, which):
+            c[k].wait_recv()
+            summed[of_group(which), :] = summed[of_group(which), :] + wacc[mine(which), at]
+
+        add_own(0, pd)
+        w = [go(summed.at[of_group(pd, *top)], x_in.at[0], 4, at_x), go(summed.at[of_group(pd, *low)], y_in.at[0], 5, at_y)]
+        add_own(1, px)
+        w.append(go(summed.at[of_group(px, *top)], x_in.at[1], 6, at_x))
+        add_own(2, py)
+        w.append(go(summed.at[of_group(py, *low)], y_in.at[1], 7, at_y))
+        add_own(3, r)
+        yield
+        w[0].wait_recv()
+        x_in[0] = x_in[0] + summed[of_group(py, *top), :]
+        wa = go(x_in.at[0], x_in.at[2], 8, at_y)
+        w[1].wait_recv()
+        y_in[0] = y_in[0] + summed[of_group(px, *low), :]
+        wb = go(y_in.at[0], y_in.at[2], 9, at_x)
+        yield
+        w[2].wait_recv()
+        w[3].wait_recv()
+        wa.wait_recv()
+        zsum[index, :top_rows, here] = (x_in[1] + summed[of_group(r, *top), :]) + x_in[2]
+        wb.wait_recv()
+        zsum[index, top_rows:, here] = (y_in[1] + summed[of_group(r, *low), :]) + y_in[2]
+        z1 = []
+        for k, z in enumerate(zs):
+            rows_at = pl.ds(pl.multiple_of(z * n2, 8), n2)
+            z1.append(go(zsum.at[index, rows_at, here], zin.at[index, k, :, here], 20 + k, (r, z * 2 + core)))
+        yield
+        acc = zsum[index, pl.ds(pl.multiple_of(chip * n2, 8), n2), here]
+        for k in range(chips - 1):
+            z1[k].wait_recv()
+            acc = acc + zin[index, k, :, here]
+        own_at = pl.ds(pl.multiple_of(base + r * n1 + chip * n2, 8), n2)
+        wsum[own_at, at] = acc * (1.0 / reps)
+        z2 = [go(wsum.at[own_at, at], wsum.at[own_at, at], 20 + chips + k, (r, z * 2 + core)) for k, z in enumerate(zs)]
+        yield
+        for copy in z2:
+            copy.wait_recv()
+
+        def share(rows_at, k, peer):
+            return go(wsum.at[rows_at, at], wsum.at[rows_at, at], k, peer)
+
+        t = [share(mine(r, *top), 10, at_x), share(mine(r, *low), 11, at_y), share(mine(r, *low), 12, at_x),
+             share(mine(r, *top), 13, at_y), share(mine(r), 14, mate)]
+        yield
+        t[0].wait_recv()
+        t.append(share(mine(px, *top), 15, at_y))
+        t[1].wait_recv()
+        t.append(share(mine(py, *low), 16, at_x))
+        yield
+        t[2].wait_recv()
+        t.append(share(mine(px), 17, mate))
+        t[3].wait_recv()
+        t.append(share(mine(py), 18, mate))
+        yield
+        t[5].wait_recv()
+        t[6].wait_recv()
+        t.append(share(mine(pd), 19, mate))
+        yield
+        for i in (4, 7, 8, 9):
+            t[i].wait_recv()
+        factor = product(inv[...], wsum[:, at])
+        fh[:, at], fl[:, at] = split(factor)
+        squares.append(jnp.sum(factor * factor, axis=1, keepdims=True))
+        yield
 
     def invert():
+        for copy in g3:
+            copy.wait_recv()
         inv[...] = yield from inverse_lower(gfull[...], rank)
         yield
 
-    steps = invert()
-    c[0].wait_recv()
-    add_own(pd)
-    w1 = [factor_to(cin.at[group_of(pd), lo], wx.at[0], 4, at_x),
-          factor_to(cin.at[group_of(pd), hi], wy.at[0], 5, at_y)]
-    c[1].wait_recv()
-    add_own(px)
-    w1.append(factor_to(cin.at[group_of(px), lo], wx.at[1], 6, at_x))
-    c[2].wait_recv()
-    add_own(py)
-    w1.append(factor_to(cin.at[group_of(py), hi], wy.at[1], 7, at_y))
-    c[3].wait_recv()
-    add_own(r)
-    for copy in g3:
-        copy.wait_recv()
-    w1[0].wait_recv()
-    wx[0] = wx[0] + cin[group_of(py), lo]
-    wa = factor_to(wx.at[0], wx2, 8, at_y)
-    w1[1].wait_recv()
-    wy[0] = wy[0] + cin[group_of(px), hi]
-    wb = factor_to(wy.at[0], wy2, 9, at_x)
-    next(steps)
-    w1[2].wait_recv()
-    wx[1] = wx[1] + cin[group_of(r), lo]
-    w1[3].wait_recv()
-    wy[1] = wy[1] + cin[group_of(r), hi]
-    wa.wait_recv()
-    zsum[:, lo] = wx[1] + wx2[...]
-    wb.wait_recv()
-    zsum[:, hi] = wy[1] + wy2[...]
-    z1 = []
-    for k, z in enumerate(zs):
-        at = pl.ds(pl.multiple_of(z * n2, 8), n2)
-        z1.append(factor_to(zsum.at[at], zin.at[k], 20 + k, (r, z * 2 + core)))
-    next(steps)
-    acc = zsum[pl.ds(pl.multiple_of(chip * n2, 8), n2), :]
-    for k in range(chips - 1):
-        z1[k].wait_recv()
-        acc = acc + zin[k]
-
-    def group(rep):
-        return pl.ds(pl.multiple_of(base + rep * n1, 8), n1)
-
-    at = pl.ds(pl.multiple_of(base + r * n1 + chip * n2, 8), n2)
-    wsum[at, :] = acc * (1.0 / reps)
-    z2 = [factor_to(wsum.at[at], wsum.at[at], 20 + chips + k, (r, z * 2 + core)) for k, z in enumerate(zs)]
-    next(steps)
-    for copy in z2:
-        copy.wait_recv()
-    gr, gx, gy, gd = group(r), group(px), group(py), group(pd)
-
-    def share(at, k, peer):
-        return factor_to(wsum.at[at], wsum.at[at], k, peer)
-
-    t = [share((gr, lo), 10, at_x), share((gr, hi), 11, at_y), share((gr, hi), 12, at_x),
-         share((gr, lo), 13, at_y), share((gr,), 14, mate)]
-    next(steps)
-    t[0].wait_recv()
-    t.append(share((gx, lo), 15, at_y))
-    t[1].wait_recv()
-    t.append(share((gy, hi), 16, at_x))
-    next(steps)
-
-    step = 256 if rows % 256 == 0 else chunk
-
-    @pl.loop(0, rows // step)
-    def _(i):
-        at = pl.ds(pl.multiple_of(i * step, 16), step)
-        qh[at, :], ql[at, :] = split(product(full[at, :], inv[...], NT))
-
-    t[2].wait_recv()
-    t.append(share((gx,), 17, mate))
-    t[3].wait_recv()
-    t.append(share((gy,), 18, mate))
-    t[5].wait_recv()
-    t[6].wait_recv()
-    t.append(share((gd,), 19, mate))
-    for index in (4, 7, 8, 9):
-        t[index].wait_recv()
-    sent = gz1 + mates + s1 + [a, b] + t1 + t2 + g1 + g2 + g3 + c + w1 + [wa, wb] + z1 + z2 + t
+    def orthonormalize():
+        step = 256 if rows % 256 == 0 else chunk
+
+        @pl.loop(0, rows // step)
+        def _(i):
+            at = pl.ds(pl.multiple_of(i * step, 16), step)
+            q[at, :] = product(full[at, :], inv[...], NT)
+
+    runs = {name: factor_sum(i) for i, name in enumerate("abcd")}
+    runs["i"] = invert()
+    terms = iter(range(streams))
+    transpose(pd)
+    for name in itertools.chain(*ORDER):
+        if name == "L":
+            i = next(terms)
+            add_term(pd, pl.ds(starts[i], widths[i]), False)
+        elif name == "q":
+            for _ in runs["i"]:
+                pass
+            orthonormalize()
+        else:
+            next(runs[name], None)
+    norms = jnp.sqrt(sum(squares) + epsilon)
+    norm[...] = jnp.broadcast_to(norms, (rank, 128)).T[:8, :]
+    sent = gz1 + mates + early + s1 + [a, b] + t1 + t2 + g1 + g2 + g3
     for copies in (ax, ay, fx, fy):
         sent += [copies[k] for k in range(chips - 1)]
-    for copy in sent:
+    for copy in sent + started:
         copy.wait_send()
 
 
-def finish(scale, shard_n, bh, bl, qh, ql, w_ref, inv, mom_ref, upd_ref, new_ref, plain, high, low, norm):
+def finish(scale, shard_n, bh, bl, q, fh, fl, norm, mom_ref, upd_ref, new_ref):
     i = pl.program_id(0)
+    rank, cols = fh.shape
 
     @pl.when(i == 0)
     def _():
-        rank, cols = plain.shape
-        factor = product(inv[...], w_ref[...])
-        norms = jnp.sqrt(jnp.sum(factor * factor, axis=1, keepdims=True) + epsilon)
-        new = factor / norms
-        norm[...] = new
-        plain[...] = ((1.0 - decay_rate) * factor).astype(bf16)
-        high[...], low[...] = split(new)
         f = lax.axis_index("fsdp")
         own = cols // shard_n
-        span = new_ref.shape[0] + 128 - math.gcd(own, 128)
+        span = own + 128 - math.gcd(own, 128)
         first = (f * own) // 128
-        window = norm[:, pl.ds(pl.multiple_of(first * 128, 128), span)]
+        at = pl.ds(pl.multiple_of(first * 128, 128), span)
+        window = fh[:, at].astype(f32) + fl[:, at].astype(f32)
         window = pltpu.roll(window, lax.rem(span - (f * own - first * 128), span), 1)
-        new_ref[...] = window[:, :own].T
+        new_ref[...] = window[:, :own].T / norm[:1, :]
 
     tile = upd_ref.shape[0]
     at = pl.ds(pl.multiple_of(i * tile, tile), tile)
-    q1, q2 = qh[at, :], ql[at, :]
-    mom_ref[0] = (bh[at, :].astype(f32) + bl[at, :].astype(f32)) - dot(q1, plain[...])
-    direction = dot(q1, high[...]) + dot(q1, low[...]) + dot(q2, high[...])
-    upd_ref[...] = (scale * direction).astype(bf16)
+    rows = q[at, :]
+    plain = ((1.0 - decay_rate) * rows).astype(bf16)
+    high, low = split(rows * (scale / norm[:1, :]))
+    mom_ref[0] = (bh[at, :].astype(f32) + bl[at, :].astype(f32)) - dot(plain, fh[...])
+    direction = dot(high, fh[...]) + dot(low, fh[...]) + dot(high, fl[...])
+    upd_ref[...] = direction.astype(bf16)
 
 
 def params(limit, **more):
@@ -443,25 +492,28 @@
     chunk, half = rows // reps, rank // 2
     n1 = rank // 2 // reps
     tile = rows // 12
+    lanes = cols // 128
+    widths = [128 * (lanes * (i + 1) // 4 - lanes * i // 4) for i in range(4)]
+    widths.sort()
+    wide = max(widths)
     vm = pltpu.VMEM
-    kept = [vm((rows, cols), bf16), vm((rows, cols), bf16), vm((rows, rank), bf16), vm((rows, rank), bf16),
-            vm((rank, cols), f32), vm((rank, rank), f32)]
+    kept = [vm((rows, cols), bf16), vm((rows, cols), bf16), vm((rows, rank), f32),
+            vm((rank, cols), bf16), vm((rank, cols), bf16), vm((8, rank), f32)]
     kept = pl.pallas_call(
-        functools.partial(reduce_all, reps, shard_n, tile),
+        functools.partial(reduce_all, reps, shard_n, tile, widths),
         out_shape=kept,
         in_specs=[pl.BlockSpec(memory_space=pl.ANY)] * 2 + [vmem], out_specs=[vmem] * 6,
         scratch_shapes=[
-            vm((3, tile, cols), f32), vm((3, tile, cols), bf16),
+            vm((rank, cols), f32), vm((rank, rank), f32), vm((3, tile, cols), f32), vm((3, tile, cols), bf16),
             vm((cols, rank), f32), vm((cols, rank), bf16), vm((cols, rank), bf16),
             vm((rows, rank), f32), vm((rows, rank), f32), vm((2 * rank, chunk), bf16), vm((rank, cols), f32),
             vm((2, chunk, half), f32), vm((2, chunk, half), f32), vm((chunk, half), f32), vm((chunk, half), f32),
             vm((rank, rank), f32), vm((shard_n - 1, rank // shard_n, rank), f32),
             vm((4, rank // shard_n, rank), f32), vm((rank, rank), f32),
-            vm((half, cols), f32), vm((2, n1, cols // 2), f32), vm((2, n1, cols // 2), f32),
-            vm((n1, cols // 2), f32), vm((n1, cols // 2), f32),
-            vm((chips - 1, n1 // chips, cols), f32), vm((n1, cols), f32),
-            dma((2, 3)), dma, dma((6 * chips,)), dma((6 * chips,)), dma((12,)), dma((12,)),
-            dma((2 * shard_n + 4,)), dma((2 * shard_n + 4,)), dma((20 + 2 * chips,)), dma((20 + 2 * chips,)),
+            vm((4, half, wide), f32), vm((4, 3, n1 // 2, wide), f32), vm((4, 3, n1 // 2, wide), f32),
+            vm((4, chips - 1, n1 // chips, wide), f32), vm((4, n1, wide), f32),
+            dma((2, 3)), dma, dma((6 * chips,)), dma((6 * chips,)), dma((14,)), dma((14,)),
+            dma((2 * shard_n + 4,)), dma((2 * shard_n + 4,)), dma((4, 20 + 2 * chips)), dma((4, 20 + 2 * chips)),
         ],
         compiler_params=params(35, collective_id=0, has_side_effects=True),
         name="reduce_all",
@@ -478,7 +530,6 @@
         in_specs=[vmem] * 6,
         out_specs=(pl.BlockSpec((1, step, cols), lambda i: (0, i, 0)), pl.BlockSpec((step, cols), lambda i: (i, 0)),
                    pl.BlockSpec((cols // shard_n, rank), lambda i: (0, 0))),
-        scratch_shapes=[vm((rank, cols), bf16)] * 3 + [vm((rank, cols), f32)],
         compiler_params=params(35), name="finish",
     )(*[pltpu.with_memory_space_constraint(x, pltpu.VMEM) for x in kept])
 
@@ -511,8 +562,8 @@
         rank = right_factor.shape[1]
         fits = (
             reps == 4 and shard_n % 2 == 0 and shard_n > 2 and rows % 1152 == 0
-            and (cols // shard_n) % 96 == 0 and cols % 256 == 0
-            and rank % (8 * reps * shard_n) == 0
+            and (cols // shard_n) % 96 == 0 and cols % 256 == 0 and cols >= 512
+            and rank % (8 * reps * shard_n) == 0 and rank % (16 * 2 * reps) == 0
         )
         run = by_kernels if fits else by_collectives
         return run(reps, shard_n, rows * shard_n, momentum, gradient, right_factor)

time: 149 us -> 123 us (0.83)
  Pallas kernels: 148 us -> 123 us
    pallas_call x1, Pallas kernels: 131 us -> 108 us  [by_kernels(): pl.pallas_call(functools.partial(reduce_all, reps, shard_n, tile, widths)...]
    pallas_call x1, Pallas kernels: 16.4 us -> 14.3 us  [by_kernels(): pl.pallas_call(functools.partial(finish, math.sqrt(total_rows * cols / ra...]
where the time goes in v2:
time: 123 us
  Pallas kernels  123 us (100%)
    pallas_call x1, Pallas kernels, by_kernels(): pl.pallas_call(functools.partial(reduce_all, reps, shard_n, tile, widths)...  108 us
    pallas_call x1, Pallas kernels, by_kernels(): pl.pallas_call(functools.partial(finish, math.sqrt(total_rows * cols / ra...  14.3 us

profile of v2, /device:TPU:1, one launch (start us, length us, event | category | flops | bytes accessed | tf_op | source)
XLA Modules:
  0.0 123.3 jit_solution(7115321173970711844)
XLA Ops:
  0.6 108.3 %reduce_all.1 = (bf16[2304,2304]{1,0:T(8,128)(2,1)S(1)}, bf16[2304,2304]{1,0:T(8,128)(2,1)S(1)}, f32[2304,256]{1,0:T(8,128)S(1)}, bf16[256,2304]{1,0:T(8,128)(2,...) custom-call(f32[1,2304,2304]{2,1,0:T(8,128)} %m_ref.1, bf16[1,2304,2304]{2,1,0:T(8,128)(2,1)} %g_ref.1, ...), custom_call_target="tpu_custom_call" | custom-call | tf_op jit(solution)/shard_map/reduce_all/pallas_call | solution.py:502
  109.0 14.3 %finish.1 = (f32[1,2304,2304]{2,1,0:T(8,128)}, bf16[2304,2304]{1,0:T(8,128)(2,1)}, f32[288,256]{1,0:T(8,128)}) custom-call(bf16[2304,2304]{1,0:T(8,128)(2,1)S(1)} %get-tuple-element.9.bh, bf16[2304,2304]{1,0:T(8,128)(2,1)S(1)} %get-tuple-element.10.bl, f32[2304,256]{1,0:T(8,128)S(1)} %get-tuple-element.11.q, bf16[256,2304]{1,0:T(8,128)(2,1)S(1)} %get-tuple-element.12.fh, ...), custom_call_target="tpu_custom_call" | custom-call | tf_op jit(solution)/shard_map/finish/pallas_call | solution.py:522

commit v3 on v2

--- a/solution.py
+++ b/solution.py
@@ -33,13 +33,6 @@
 
 NT = (((1,), (1,)), ((), ()))
 TN = (((0,), (0,)), ((), ()))
-
-
-def greet(peers):
-    barrier = pltpu.get_barrier_semaphore()
-    for peer in peers:
-        pl.semaphore_signal(barrier, inc=1, device_id=peer, device_id_type=MESH)
-    pl.semaphore_wait(barrier, len(peers))
 
 
 def remote(src, dst, send_sem, recv_sem, peer):
@@ -125,14 +118,20 @@
         return (pltpu.make_async_copy(m_ref.at[0, at], ms.at[slot], lsem.at[0, slot]),
                 pltpu.make_async_copy(g_ref.at[0, at], gs.at[slot], lsem.at[1, slot]))
 
+    def block(index):
+        return pl.ds(pl.multiple_of(index * own_rows, 8), own_rows)
+
+    barrier = pltpu.get_barrier_semaphore()
+    known = [at_x, at_y, (pd, f)] + [(r, lax.rem(f + k, shard_n)) for k in range(1, shard_n)]
+    for peer in known:
+        pl.semaphore_signal(barrier, inc=1, device_id=peer, device_id_type=MESH)
+    local = pltpu.make_async_copy(own_ref, rfull.at[block(f)], own_sem)
+    local.start()
     for t in range(slots):
         for copy in load(t):
             copy.start()
-
-    greet([at_x, at_y, (pd, f)] + [(r, lax.rem(f + k, shard_n)) for k in range(1, shard_n)])
-
-    def block(index):
-        return pl.ds(pl.multiple_of(index * own_rows, 8), own_rows)
+    local.wait()
+    pl.semaphore_wait(barrier, len(known))
 
     quarter = own_rows // reps
 
@@ -142,12 +141,16 @@
     def rsend_to(src, dst, k, peer):
         return remote(src, dst, rsend.at[k], rrecv.at[k], peer)
 
-    local = pltpu.make_async_copy(own_ref, rfull.at[block(f)], own_sem)
-    local.start()
-    gz1 = [rsend_to(own_ref.at[pl.ds(pl.multiple_of(r * quarter, 8), quarter)], rfull.at[part_of(f, r)], k,
-                    (r, lax.rem(chip + k + 1, chips) * 2 + core)) for k in range(chips - 1)]
-    mates = [rsend_to(own_ref, rfull.at[block(f)], chips, mate)]
-    source = [lax.rem(chip + chips - k - 1, chips) * 2 + core for k in range(chips - 1)]
+    if chips == 4:
+        ahead = [chip + 1 - 2 * lax.rem(chip, 2), 3 - chip, lax.rem(chip + 2, 4)]
+        behind = ahead
+    else:
+        ahead = [lax.rem(chip + k, chips) for k in range(1, chips)]
+        behind = [lax.rem(chip + chips - k, chips) for k in range(1, chips)]
+    mine = rfull.at[part_of(f, r)]
+    gz1 = [rsend_to(mine, mine, k, (r, z * 2 + core)) for k, z in enumerate(ahead)]
+    mates = [rsend_to(rfull.at[block(f)], rfull.at[block(f)], chips, mate)]
+    source = [z * 2 + core for z in behind]
     ax, ay, fx, fy = {}, {}, {}, {}
 
     def spread(k):
@@ -196,7 +199,6 @@
         at = pl.ds(pl.multiple_of(index * own_rows, 16), own_rows)
         rh[at, :], rl[at, :] = split(rfull[at, :])
 
-    local.wait()
     split_rows(f)
     mates[0].wait_recv()
     split_rows(chip * 2 + 1 - core)
@@ -205,7 +207,7 @@
         split_rows(source[k])
     for k in range(chips - 1):
         mates[k + 1].wait_recv()
-        split_rows(lax.rem(chip + chips - k - 1, chips) * 2 + 1 - core)
+        split_rows(behind[k] * 2 + 1 - core)
 
     def of(index):
         return pl.ds(pl.multiple_of(index * chunk, 16), chunk)
@@ -502,7 +504,7 @@
     kept = pl.pallas_call(
         functools.partial(reduce_all, reps, shard_n, tile, widths),
         out_shape=kept,
-        in_specs=[pl.BlockSpec(memory_space=pl.ANY)] * 2 + [vmem], out_specs=[vmem] * 6,
+        in_specs=[pl.BlockSpec(memory_space=pl.ANY)] * 3, out_specs=[vmem] * 6,
         scratch_shapes=[
             vm((rank, cols), f32), vm((rank, rank), f32), vm((3, tile, cols), f32), vm((3, tile, cols), bf16),
             vm((cols, rank), f32), vm((cols, rank), bf16), vm((cols, rank), bf16),
@@ -518,7 +520,7 @@
         compiler_params=params(35, collective_id=0, has_side_effects=True),
         name="reduce_all",
     )(momentum, gradient, right_factor)
-    step = 256 if rows % 256 == 0 else rows // 8
+    step = rows // 6
     return pl.pallas_call(
         functools.partial(finish, math.sqrt(total_rows * cols / rank), shard_n),
         grid=(rows // step,),

time: 123 us -> 121 us (0.984)
  Pallas kernels: 123 us -> 121 us
    pallas_call x1, Pallas kernels: 108 us -> 107 us  [by_kernels(): pl.pallas_call(functools.partial(reduce_all, reps, shard_n, tile, widths)...]
where the time goes in v3:
time: 121 us
  Pallas kernels  121 us (100%)
    pallas_call x1, Pallas kernels, by_kernels(): pl.pallas_call(functools.partial(reduce_all, reps, shard_n, tile, widths)...  107 us
    pallas_call x1, Pallas kernels, by_kernels(): pl.pallas_call(functools.partial(finish, math.sqrt(total_rows * cols / ra...  14 us

profile of v3, /device:TPU:1, one launch (start us, length us, event | category | flops | bytes accessed | tf_op | source)
XLA Modules:
  0.0 121.2 jit_solution(459049811347983929)
XLA Ops:
  0.6 106.5 %reduce_all.1 = (bf16[2304,2304]{1,0:T(8,128)(2,1)S(1)}, bf16[2304,2304]{1,0:T(8,128)(2,1)S(1)}, f32[2304,256]{1,0:T(8,128)S(1)}, bf16[256,2304]{1,0:T(8,128)(2,...) custom-call(f32[1,2304,2304]{2,1,0:T(8,128)} %m_ref.1, bf16[1,2304,2304]{2,1,0:T(8,128)(2,1)} %g_ref.1, ...), custom_call_target="tpu_custom_call" | custom-call | tf_op jit(solution)/shard_map/reduce_all/pallas_call | solution.py:504
  107.2 14.0 %finish.1 = (f32[1,2304,2304]{2,1,0:T(8,128)}, bf16[2304,2304]{1,0:T(8,128)(2,1)}, f32[288,256]{1,0:T(8,128)}) custom-call(bf16[2304,2304]{1,0:T(8,128)(2,1)S(1)} %get-tuple-element.9.bh, bf16[2304,2304]{1,0:T(8,128)(2,1)S(1)} %get-tuple-element.10.bl, f32[2304,256]{1,0:T(8,128)S(1)} %get-tuple-element.11.q, bf16[256,2304]{1,0:T(8,128)(2,1)S(1)} %get-tuple-element.12.fh, ...), custom_call_target="tpu_custom_call" | custom-call | tf_op jit(solution)/shard_map/finish/pallas_call | solution.py:524

commit v4 on v3

--- a/solution.py
+++ b/solution.py
@@ -243,24 +243,29 @@
     early[0].wait_recv()
     s1[0].wait_recv()
     xin[0] = xin[0] + part[of(py), left]
-    a = exchange(xin.at[0], xin2, 4, at_y)
+    parts = [pl.ds(0, half_rows), pl.ds(half_rows, half_rows)]
+    a = [exchange(xin.at[0, at], xin2.at[at], k, at_y) for k, at in zip((4, 14), parts)]
     early[1].wait_recv()
     s1[1].wait_recv()
     yin[0] = yin[0] + part[of(px), right]
-    b = exchange(yin.at[0], yin2, 5, at_x)
+    b = [exchange(yin.at[0, at], yin2.at[at], k, at_x) for k, at in zip((5, 15), parts)]
     project(r)
     s1[2].wait_recv()
     xin[1] = xin[1] + part[of(r), left]
     s1[3].wait_recv()
     yin[1] = yin[1] + part[of(r), right]
-    a.wait_recv()
-    full[of(r), left] = xin[1] + xin2[...]
-    b.wait_recv()
-    full[of(r), right] = yin[1] + yin2[...]
     whole = of(r)
-    t1 = [
-        exchange(full.at[whole, left], full.at[whole, left], 6, at_x),
-        exchange(full.at[whole, right], full.at[whole, right], 7, at_y),
+    t1 = []
+    for i, at in enumerate(parts):
+        here = half_of(r, i)
+        a[i].wait_recv()
+        full[here, left] = xin[1, at, :] + xin2[at, :]
+        t1.append(exchange(full.at[here, left], full.at[here, left], (6, 16)[i], at_x))
+        b[i].wait_recv()
+        full[here, right] = yin[1, at, :] + yin2[at, :]
+        t1.append(exchange(full.at[here, right], full.at[here, right], (7, 17)[i], at_y))
+    late = t1[2:]
+    t1 = t1[:2] + [
         exchange(full.at[whole, right], full.at[whole, right], 8, at_x),
         exchange(full.at[whole, left], full.at[whole, left], 9, at_y),
     ]
@@ -304,8 +309,10 @@
     gz[0] = acc
     g2 = [gram_to(gz.at[0], gz.at[k + 1], shard_n + k, peer) for k, peer in enumerate((at_x, at_y, (pd, f)))]
     t1[0].wait_recv()
+    late[0].wait_recv()
     t2 = [exchange(full.at[of(px), left], full.at[of(px), left], 10, at_y)]
     t1[1].wait_recv()
+    late[1].wait_recv()
     t2.append(exchange(full.at[of(py), right], full.at[of(py), right], 11, at_x))
     t1[2].wait_recv()
     left_factor(px, False)
@@ -449,7 +456,7 @@
             next(runs[name], None)
     norms = jnp.sqrt(sum(squares) + epsilon)
     norm[...] = jnp.broadcast_to(norms, (rank, 128)).T[:8, :]
-    sent = gz1 + mates + early + s1 + [a, b] + t1 + t2 + g1 + g2 + g3
+    sent = gz1 + mates + early + s1 + a + b + late + t1 + t2 + g1 + g2 + g3
     for copies in (ax, ay, fx, fy):
         sent += [copies[k] for k in range(chips - 1)]
     for copy in sent + started:
@@ -514,7 +521,7 @@
             vm((4, rank // shard_n, rank), f32), vm((rank, rank), f32),
             vm((4, half, wide), f32), vm((4, 3, n1 // 2, wide), f32), vm((4, 3, n1 // 2, wide), f32),
             vm((4, chips - 1, n1 // chips, wide), f32), vm((4, n1, wide), f32),
-            dma((2, 3)), dma, dma((6 * chips,)), dma((6 * chips,)), dma((14,)), dma((14,)),
+            dma((2, 3)), dma, dma((6 * chips,)), dma((6 * chips,)), dma((18,)), dma((18,)),
             dma((2 * shard_n + 4,)), dma((2 * shard_n + 4,)), dma((4, 20 + 2 * chips)), dma((4, 20 + 2 * chips)),
         ],
         compiler_params=params(35, collective_id=0, has_side_effects=True),

time: 121 us -> 120 us (level)
  Pallas kernels: 121 us -> 119 us
    pallas_call x1, Pallas kernels: 107 us -> 105 us  [by_kernels(): pl.pallas_call(functools.partial(reduce_all, reps, shard_n, tile, widths)...]
where the time goes in v4:
time: 120 us
  Pallas kernels  119 us (99%)
    pallas_call x1, Pallas kernels, by_kernels(): pl.pallas_call(functools.partial(reduce_all, reps, shard_n, tile, widths)...  105 us
    pallas_call x1, Pallas kernels, by_kernels(): pl.pallas_call(functools.partial(finish, math.sqrt(total_rows * cols / ra...  14 us

profile of v4, /device:TPU:1, one launch (start us, length us, event | category | flops | bytes accessed | tf_op | source)
XLA Modules:
  0.0 119.8 jit_solution(3206074642534382523)
XLA Ops:
  0.6 105.1 %reduce_all.1 = (bf16[2304,2304]{1,0:T(8,128)(2,1)S(1)}, bf16[2304,2304]{1,0:T(8,128)(2,1)S(1)}, f32[2304,256]{1,0:T(8,128)S(1)}, bf16[256,2304]{1,0:T(8,128)(2,...) custom-call(f32[1,2304,2304]{2,1,0:T(8,128)} %m_ref.1, bf16[1,2304,2304]{2,1,0:T(8,128)(2,1)} %g_ref.1, ...), custom_call_target="tpu_custom_call" | custom-call | tf_op jit(solution)/shard_map/reduce_all/pallas_call | solution.py:511
  105.8 14.0 %finish.1 = (f32[1,2304,2304]{2,1,0:T(8,128)}, bf16[2304,2304]{1,0:T(8,128)(2,1)}, f32[288,256]{1,0:T(8,128)}) custom-call(bf16[2304,2304]{1,0:T(8,128)(2,1)S(1)} %get-tuple-element.9.bh, bf16[2304,2304]{1,0:T(8,128)(2,1)S(1)} %get-tuple-element.10.bl, f32[2304,256]{1,0:T(8,128)S(1)} %get-tuple-element.11.q, bf16[256,2304]{1,0:T(8,128)(2,1)S(1)} %get-tuple-element.12.fh, ...), custom_call_target="tpu_custom_call" | custom-call | tf_op jit(solution)/shard_map/finish/pallas_call | solution.py:531
